TPU v7x, 32 devices: a whole 2x2x4 slice. The times are simulated.
32 devices in a mesh: dp: 8 (over y, x, core), seq: 4 (over z).
Axes of the slice: x: 2, y: 2, z: 4, core: 2. Of those that a mesh axis runs over, the one named last changes fastest.
Arguments:
- tokens: bfloat16 [8, 512, 2048], P('dp', 'seq'), may hold values from -6 to 6
- qkv_weight: bfloat16 [3, 2048, 1024], P(None, 'dp', 'seq'), may hold values from -0.125 to 0.125
- qk_scale: float32 [1024], replicated, may hold values from 0.5 to 10
- out_weight: bfloat16 [1024, 2048], P('seq', 'dp'), may hold values from -0.1875 to 0.1875
- mix_rates: float32 [2, 2048], replicated, may hold values from 0.1 to 0.6
- gate_up_weight: bfloat16 [2, 2048, 8192], P(None, 'dp', 'seq'), may hold values from -0.125 to 0.125
- mlp_scales: float32 [2, 8192], P(None, 'seq'), may hold values from 0.5 to 2
- down_weight: bfloat16 [8192, 2048], P('seq', 'dp'), may hold values from -0.0625 to 0.0625
Outputs:
- result: bfloat16 [8, 512, 2048], P('dp', 'seq')
All inputs are finite; a program needn't handle non-finite values.
Results may differ from a plain program's by a relative error of at most 0.015.
The roundings to bfloat16 on the way count: a program that leaves them out, or rounds other values in their place, can miss the bound.
Values may be sent and summed in bfloat16 or wider, within the bound.
No kernel may reach another device: no remote copies, remote signals or barrier semaphores. Data moves between devices by JAX's collectives and lax.ppermute only.
A program may use at most 128 MiB of HBM per device.

v0:
```python
import jax
import jax.numpy as jnp
from jax import lax
from jax.sharding import PartitionSpec as P

HD = 128


def unit_rms(values_in):
    return values_in * lax.rsqrt(jnp.mean(values_in * values_in, axis=-1, keepdims=True) + 1e-06)


def prepare(projected, scale_heads):
    queries = unit_rms(projected[:, 0]) * scale_heads
    key_rows = unit_rms(projected[:, 1]) * scale_heads
    return jnp.stack([queries, key_rows, projected[:, 2]], axis=1).astype(jnp.bfloat16)


def attend(stacked):
    length = stacked.shape[0]
    head_count = stacked.shape[2]
    head_dim = stacked.shape[3]
    block_rows = min(length, 512)
    block_count = length // block_rows
    key_rows = stacked[:, 1]
    value_rows = stacked[:, 2]
    queries = stacked[:, 0].reshape(block_count, block_rows, head_count, head_dim)
    positions = jnp.arange(length, dtype=jnp.int32)
    factor = head_dim ** (-0.5)

    def one_block(inputs):
        block_index, query_block = inputs
        scores = (
            jnp.einsum("qhd,khd->hqk", query_block, key_rows, preferred_element_type=jnp.float32)
            * factor
        )
        query_pos = block_index * block_rows + jnp.arange(block_rows, dtype=jnp.int32)
        allowed = positions[None, :] <= query_pos[:, None]
        scores = jnp.where(allowed[None], scores, -1e30)
        highest = jnp.max(scores, axis=-1, keepdims=True)
        powers = jnp.exp(scores - highest)
        shares = (powers / jnp.sum(powers, axis=-1, keepdims=True)).astype(jnp.bfloat16)
        mixed = jnp.einsum("hqk,khd->qhd", shares, value_rows, preferred_element_type=jnp.float32)
        return mixed.astype(jnp.bfloat16)

    mixed_all = lax.map(one_block, (jnp.arange(block_count, dtype=jnp.int32), queries))
    return mixed_all.reshape(length, head_count, head_dim)


def on_device(
    tokens, qkv_weight, qk_scale, out_weight, mix_rates, gate_up_weight, mlp_scales, down_weight
):
    own_rows = tokens[0]
    head_dim = HD
    normed = unit_rms(own_rows.astype(jnp.float32)).astype(jnp.bfloat16)
    scale_all = qk_scale.reshape(-1, head_dim)
    sequence = lax.all_gather(normed, "seq", axis=0, tiled=True)
    length = sequence.shape[0]
    columns = sequence
    projected = jnp.einsum(
        "td,cdn->tcn",
        columns,
        lax.all_gather(qkv_weight, "dp", axis=1, tiled=True),
        preferred_element_type=jnp.float32,
    )
    local_heads = qkv_weight.shape[2] // head_dim
    scale_local = lax.dynamic_slice_in_dim(
        scale_all, lax.axis_index("seq") * local_heads, local_heads, 0
    )
    stacked = prepare(projected.reshape(length, 3, local_heads, head_dim), scale_local)
    attended = attend(stacked).reshape(length, -1)
    out_cols_all = lax.all_gather(out_weight, "dp", axis=1, tiled=True)
    part_rows = attended
    attention = lax.psum_scatter(
        jnp.dot(part_rows, out_cols_all, preferred_element_type=jnp.float32).astype(jnp.bfloat16),
        "seq",
        scatter_dimension=0,
        tiled=True,
    ).astype(jnp.float32)
    normed_f = normed.astype(jnp.float32)
    middle = unit_rms(normed_f + mix_rates[0] * (unit_rms(attention) - normed_f)).astype(
        jnp.bfloat16
    )
    sequence_mid = lax.all_gather(middle, "seq", axis=0, tiled=True)
    columns = sequence_mid
    gate_up = jnp.einsum(
        "td,cdf->tcf",
        columns,
        lax.all_gather(gate_up_weight, "dp", axis=1, tiled=True),
        preferred_element_type=jnp.float32,
    )
    hidden = (jax.nn.silu(gate_up[:, 0] * mlp_scales[0]) * (gate_up[:, 1] * mlp_scales[1])).astype(
        jnp.bfloat16
    )
    down_all = lax.all_gather(down_weight, "dp", axis=1, tiled=True)
    part_rows = hidden
    feed_out = lax.psum_scatter(
        jnp.dot(part_rows, down_all, preferred_element_type=jnp.float32).astype(jnp.bfloat16),
        "seq",
        scatter_dimension=0,
        tiled=True,
    ).astype(jnp.float32)
    middle_f = middle.astype(jnp.float32)
    result = unit_rms(middle_f + mix_rates[1] * (unit_rms(feed_out) - middle_f)).astype(
        jnp.bfloat16
    )
    return result[None]


def solution(mesh):
    return jax.shard_map(
        on_device,
        mesh=mesh,
        in_specs=(
            P("dp", "seq", None),
            P(None, "dp", "seq"),
            P(),
            P("seq", "dp"),
            P(),
            P(None, "dp", "seq"),
            P(None, "seq"),
            P("seq", "dp"),
        ),
        out_specs=P("dp", "seq", None),
        check_vma=False,
    )
```

profile of v0, /device:TPU:0, one launch (start us, length us, event | category | flops | bytes accessed | tf_op | source)
XLA Modules:
  0.0 430.2 jit_solution(14153458220697589885)
XLA Ops:
  6.5 1.3 fusion.17
  7.8 2.0 fusion.18
  9.9 0.9 copy.9
  11.8 46.6 %all-gather.7.cloned.1.call-done = bf16[512,2048]{1,0:T(8,128)(2,1)} async-done(((bf16[128,2048]{1,0:T(8,128)(2,1)}), bf16[512,2048]{1,0:T(8,128)(2,1)}) %all-gather.7.cloned.1.call-update) | async-done | bytes 2097168 | tf_op jit(solution)/shard_map/all_gather | solution.py:57
  58.4 33.4 %all-gather.9.cloned.1.call-done = bf16[3,2048,256]{1,2,0:T(8,128)(2,1)} async-done(((bf16[3,256,256]{1,2,0:T(8,128)(2,1)}), bf16[3,2048,256]{1,2,0:T(8,128)(2,1)}) %all-gather.9.cloned.1.call-update) | async-done | bytes 3145744 | tf_op jit(solution)/shard_map/all_gather | solution.py:63
  91.8 4.3 %fusion.7 = f32[512,3,256]{0,2,1:T(8,128)S(1)} fusion(bf16[3,2048,256]{1,2,0:T(8,128)(2,1)} %all-gather.9.cloned.1.call-done, bf16[512,2048]{1,0:T(8,128)(2,1)} %all-gather.7.cloned.1.call-done), kind=kOutput, calls=%fused_computation.11 | convolution fusion | flops 1610612736 | bytes 6815744 | tf_op jit(solution)/shard_map/td,cdn->tcn/dot_general | solution.py:60
  96.3 1.1 fusion.63
  97.4 1.3 convolution_convert_fusion.2
  98.7 18.5 %all-gather.11.cloned.1.call-done = bf16[256,2048]{1,0:T(8,128)(2,1)} async-done(((bf16[256,256]{1,0:T(8,128)(2,1)}), bf16[256,2048]{1,0:T(8,128)(2,1)}) %all-gather.11.cloned.1.call-update) | async-done | bytes 1048592 | tf_op jit(solution)/shard_map/all_gather | solution.py:72
  117.2 3.3 convolution_convert_fusion
  121.3 43.1 %reduce-scatter.3.cloned.1.call-done = bf16[128,2048]{1,0:T(8,128)(2,1)} async-done(((bf16[512,2048]{1,0:T(8,128)(2,1)}), bf16[128,2048]{1,0:T(8,128)(2,1)}) %reduce-scatter.3.cloned.1.call-update) | async-done | bytes 524304 | tf_op jit(solution)/shard_map/reduce_scatter | solution.py:74
  164.4 1.2 fusion.14
  165.6 1.5 multiply_reduce_fusion.1
  167.1 2.2 multiply_convert_fusion.1
  170.0 0.7 all-gather.17.cloned.1.call-update
  171.0 43.4 %all-gather.13.cloned.1.call-done = bf16[512,2048]{1,0:T(8,128)(2,1)} async-done(((bf16[128,2048]{1,0:T(8,128)(2,1)}), bf16[512,2048]{1,0:T(8,128)(2,1)}) %all-gather.13.cloned.1.call-update) | async-done | bytes 2097168 | tf_op jit(solution)/shard_map/all_gather | solution.py:84
  214.4 90.3 %all-gather.15.cloned.1.call-done = bf16[2,2048,2048]{2,1,0:T(8,128)(2,1)} async-done(((bf16[2,256,2048]{2,1,0:T(8,128)(2,1)}), bf16[2,2048,2048]{2,1,0:T(8,128)(2,1)}) %all-gather.15.cloned.1.call-update) | async-done | bytes 16777232 | tf_op jit(solution)/shard_map/all_gather | solution.py:89
  304.7 14.9 %fusion.5 = f32[512,2,2048]{2,0,1:T(8,128)} fusion(bf16[2,2048,2048]{2,1,0:T(8,128)(2,1)} %all-gather.15.cloned.1.call-done, bf16[512,2048]{1,0:T(8,128)(2,1)} %all-gather.13.cloned.1.call-done), kind=kOutput, calls=%fused_computation.9 | convolution fusion | flops 8589934592 | bytes 27262976 | tf_op jit(solution)/shard_map/td,cdf->tcf/dot_general | solution.py:86
  319.6 42.9 %all-gather.17.cloned.1.call-done = bf16[2048,2048]{1,0:T(8,128)(2,1)} async-done(((bf16[2048,256]{1,0:T(8,128)(2,1)}), bf16[2048,2048]{1,0:T(8,128)(2,1)}) %all-gather.17.cloned.1.call-update) | async-done | bytes 8388624 | tf_op jit(solution)/shard_map/all_gather | solution.py:95
  362.5 11.9 %convolution_convert_fusion.1 = bf16[512,2048]{1,0:T(8,128)(2,1)} fusion(bf16[2048,2048]{1,0:T(8,128)(2,1)} %all-gather.17.cloned.1.call-done, f32[512,2,2048]{2,0,1:T(8,128)} %fusion.5, f32[2048]{0:T(1024)S(1)} %bitcast.89, f32[2048]{0:T(1024)S(1)} %bitcast.88), kind=kOutput, calls=%fused_computation.8 | convolution fusion | flops 4304404480 | bytes 18890752 | tf_op jit(solution)/shard_map/dot_general | solution.py:98
  374.4 43.8 %reduce-scatter.5.cloned.1.call-done = bf16[128,2048]{1,0:T(8,128)(2,1)} async-done(((bf16[512,2048]{1,0:T(8,128)(2,1)}), bf16[128,2048]{1,0:T(8,128)(2,1)}) %reduce-scatter.5.cloned.1.call-update) | async-done | bytes 524304 | tf_op jit(solution)/shard_map/reduce_scatter | solution.py:97
  418.2 1.2 fusion.16
  419.5 1.5 multiply_reduce_fusion
  421.0 2.3 fusion.22
  (38 shorter events, 2.7 us)
Async XLA Ops:
  6.5 5.1 %copy-start = (f32[1024]{0:T(1024)S(1)}, f32[1024]{0:T(1024)}, u32[]{:S(2)}) copy-start(f32[1024]{0:T(1024)} %param.10) | copy-start | bytes 12292
  6.5 3.4 copy-start.3
  6.5 51.8 %all-gather.7.cloned.1.call-start = ((), (), s32[]{:S(2)}) async-start(), calls=%async_computation.2 | async-start | bytes 2621440 | tf_op jit(solution)/shard_map/all_gather | solution.py:57
  9.8 82.0 %all-gather.9.cloned.1.call-start = ((), (), s32[]{:S(2)}) async-start(), calls=%async_computation.3 | async-start | bytes 3538944 | tf_op jit(solution)/shard_map/all_gather | solution.py:63
  10.9 106.3 %all-gather.11.cloned.1.call-start = ((), (), s32[]{:S(2)}) async-start(), calls=%async_computation.4 | async-start | bytes 1179648 | tf_op jit(solution)/shard_map/all_gather | solution.py:72
  11.6 152.7 %reduce-scatter.3.cloned.1.call-start = ((), (), s32[]{:S(2)}) async-start(), calls=%async_computation.5 | async-start | bytes 2621440 | tf_op jit(solution)/shard_map/reduce_scatter | solution.py:74
  120.5 0.7 copy-start.4
  120.5 45.1 %copy-start.1 = (bf16[1,128,2048]{2,1,0:T(8,128)(2,1)S(1)}, bf16[1,128,2048]{2,1,0:T(8,128)(2,1)}, u32[]{:S(2)}) copy-start(bf16[1,128,2048]{2,1,0:T(8,128)(2,1)} %param.8) | copy-start | bytes 1572868
  120.6 93.8 %all-gather.13.cloned.1.call-start = ((), (), s32[]{:S(2)}) async-start(), calls=%async_computation.6 | async-start | bytes 2621440 | tf_op jit(solution)/shard_map/all_gather | solution.py:84
  169.3 1.6 copy-start.5
  169.4 135.3 %all-gather.15.cloned.1.call-start = ((), (), s32[]{:S(2)}) async-start(), calls=%async_computation.7 | async-start | bytes 18874368 | tf_op jit(solution)/shard_map/all_gather | solution.py:89
  169.9 192.5 %all-gather.17.cloned.1.call-start = ((), (), s32[]{:S(2)}) async-start(), calls=%async_computation.8 | async-start | bytes 9437184 | tf_op jit(solution)/shard_map/all_gather | solution.py:95
  170.7 247.5 %reduce-scatter.5.cloned.1.call-start = ((), (), s32[]{:S(2)}) async-start(), calls=%async_computation.9 | async-start | bytes 2621440 | tf_op jit(solution)/shard_map/reduce_scatter | solution.py:97
  374.4 45.1 %copy-start.2 = (bf16[128,2048]{1,0:T(8,128)(2,1)S(1)}, bf16[128,2048]{1,0:T(8,128)(2,1)}, u32[]{:S(2)}) copy-start(bf16[128,2048]{1,0:T(8,128)(2,1)} %multiply_convert_fusion.1) | copy-start | bytes 1572868
Sparse Core Ops, SparseCore 0:
  10.0 48.3 all-gather.6
  60.3 31.5 all-gather.8
  93.7 23.4 all-gather.10
  120.7 43.6 reduce-scatter.2
  169.5 44.8 all-gather.12
  216.1 88.5 all-gather.14
  306.6 55.8 all-gather.16
  374.5 43.6 reduce-scatter.4
where the time goes:
time: 431 us; the launch traced here: 430 us
  waiting for transfers between devices  364 us (84%)
  matrix products  36.9 us (9%)
  between operations  13.6 us (3%)
  other arithmetic  13.5 us (3%)
    all_gather x1, waiting for transfers between devices, on_device(): lax.all_gather(gate_up_weight, 'dp', axis=1, tiled=True)  90.3 us
    all_gather x1, waiting for transfers between devices, on_device(): sequence = lax.all_gather(normed, 'seq', axis=0, tiled=True)  46.6 us
    reduce_scatter x1, waiting for transfers between devices, on_device(): lax.psum_scatter(jnp.dot(part_rows, down_all, preferred_element_type=jnp....  43.8 us
    all_gather x1, waiting for transfers between devices, on_device(): sequence_mid = lax.all_gather(middle, 'seq', axis=0, tiled=True)  43.4 us
    reduce_scatter x1, waiting for transfers between devices, on_device(): lax.psum_scatter(jnp.dot(part_rows, out_cols_all, preferred_element_type=...  43.1 us
    all_gather x1, waiting for transfers between devices, on_device(): down_all = lax.all_gather(down_weight, 'dp', axis=1, tiled=True)  42.9 us
    all_gather x1, waiting for transfers between devices, on_device(): lax.all_gather(qkv_weight, 'dp', axis=1, tiled=True)  33.4 us
    all_gather x1, waiting for transfers between devices, on_device(): out_cols_all = lax.all_gather(out_weight, 'dp', axis=1, tiled=True)  18.5 us
  transfers between devices with their start and end apart: 8, of which 8 were waited for; matrix products, arithmetic and copies ran while one was open for 5% of the time, Pallas kernels for 0%

commit v1 on v0

--- a/solution.py
+++ b/solution.py
@@ -4,6 +4,22 @@
 from jax.sharding import PartitionSpec as P
 
 HD = 128
+
+
+def product_in_turn(x, axis, dim, product):
+    peers, position, width = (lax.axis_size(axis), lax.axis_index(axis), x.shape[dim])
+    right = [(i, (i + 1) % peers) for i in range(peers)]
+    left = [(i, (i - 1) % peers) for i in range(peers)]
+    halfway = peers // 2
+    from_left = from_right = x
+    total = product(x, position * width)
+    for step in range(1, halfway + 1):
+        from_left = lax.ppermute(from_left, axis, right)
+        if step < peers - halfway:
+            from_right = lax.ppermute(from_right, axis, left)
+            total = total + product(from_right, (position + step) % peers * width)
+        total = total + product(from_left, (position - step) % peers * width)
+    return total
 
 
 def unit_rms(values_in):
@@ -83,11 +99,16 @@
     )
     sequence_mid = lax.all_gather(middle, "seq", axis=0, tiled=True)
     columns = sequence_mid
-    gate_up = jnp.einsum(
-        "td,cdf->tcf",
-        columns,
-        lax.all_gather(gate_up_weight, "dp", axis=1, tiled=True),
-        preferred_element_type=jnp.float32,
+    gate_up = product_in_turn(
+        gate_up_weight,
+        "dp",
+        1,
+        lambda part, offset: jnp.einsum(
+            "td,cdf->tcf",
+            lax.dynamic_slice_in_dim(columns, offset, part.shape[1], axis=1),
+            part,
+            preferred_element_type=jnp.float32,
+        ),
     )
     hidden = (jax.nn.silu(gate_up[:, 0] * mlp_scales[0]) * (gate_up[:, 1] * mlp_scales[1])).astype(
         jnp.bfloat16

time: 431 us -> 480 us (1.11)
  matrix products: 36.9 us -> 85.4 us
  waiting for transfers between devices: 364 us -> 356 us
  starting transfers between devices: 0.46 us -> 7.18 us
    ppermute x0 -> x7, waiting for transfers between devices: none -> 163 us  [the longest x4 160 us: product_in_turn(): from_left = lax.ppermute(from_left, axis, right)]
    all_gather x1 -> x0, waiting for transfers between devices: 90.3 us -> none  [on_device(): lax.all_gather(gate_up_weight, 'dp', axis=1, tiled=True)]
    dot_general x1 -> x8, matrix products: 14.9 us -> 63.3 us  [on_device(): jnp.einsum('td,cdf->tcf', lax.dynamic_slice_in_dim(columns, offset, part....]
    all_gather x1, waiting for transfers between devices: 43.4 us -> 0.01 us  [on_device(): sequence_mid = lax.all_gather(middle, 'seq', axis=0, tiled=True)]
    all_gather x1, waiting for transfers between devices: 42.9 us -> 0.01 us  [on_device(): down_all = lax.all_gather(down_weight, 'dp', axis=1, tiled=True)]
    ppermute x0 -> x7, starting transfers between devices: none -> 6.93 us  [the longest x3 6.87 us: product_in_turn(): from_right = lax.ppermute(from_right, axis, left)]
    reduce_scatter x1, waiting for transfers between devices: 43.8 us -> 50.1 us  [on_device(): lax.psum_scatter(jnp.dot(part_rows, down_all, preferred_element_type=jnp....]
  transfers between devices with their start and end apart: 8 -> 14, of which waited for: 8 -> 9; matrix products, arithmetic and copies ran while one was open for 5% -> 15% of each run, Pallas kernels for 0% -> 0%
where the time goes in v1:
time: 480 us; the launch traced here: 479 us
  waiting for transfers between devices  356 us (74%)
  matrix products  85.4 us (18%)
  other arithmetic  13.7 us (3%)
  between operations  13.6 us (3%)
  starting transfers between devices  7.18 us (1%)
    ppermute x4, waiting for transfers between devices, product_in_turn(): from_left = lax.ppermute(from_left, axis, right)  160 us
    dot_general x8, matrix products, on_device(): jnp.einsum('td,cdf->tcf', lax.dynamic_slice_in_dim(columns, offset, part....  63.3 us
    reduce_scatter x1, waiting for transfers between devices, on_device(): lax.psum_scatter(jnp.dot(part_rows, down_all, preferred_element_type=jnp....  50.1 us
    all_gather x1, waiting for transfers between devices, on_device(): sequence = lax.all_gather(normed, 'seq', axis=0, tiled=True)  46.6 us
    reduce_scatter x1, waiting for transfers between devices, on_device(): lax.psum_scatter(jnp.dot(part_rows, out_cols_all, preferred_element_type=...  43.1 us
    all_gather x1, waiting for transfers between devices, on_device(): lax.all_gather(qkv_weight, 'dp', axis=1, tiled=True)  33.4 us
    all_gather x1, waiting for transfers between devices, on_device(): out_cols_all = lax.all_gather(out_weight, 'dp', axis=1, tiled=True)  18.5 us
    dot_general x1, matrix products, on_device(): jnp.dot(part_rows, down_all, preferred_element_type=jnp.float32)  12 us
  transfers between devices with their start and end apart: 14, of which 9 were waited for; matrix products, arithmetic and copies ran while one was open for 15% of the time, Pallas kernels for 0%

profile of v1, /device:TPU:0, one launch (start us, length us, event | category | flops | bytes accessed | tf_op | source)
XLA Modules:
  0.0 479.0 jit_solution(10140182769900644422)
XLA Ops:
  11.8 46.6 %all-gather.6.cloned.1.call-done = bf16[512,2048]{1,0:T(8,128)(2,1)} async-done(((bf16[128,2048]{1,0:T(8,128)(2,1)}), bf16[512,2048]{1,0:T(8,128)(2,1)}) %all-gather.6.cloned.1.call-update) | async-done | bytes 2097168 | tf_op jit(solution)/shard_map/all_gather | solution.py:73
  58.4 33.4 %all-gather.8.cloned.1.call-done = bf16[3,2048,256]{1,2,0:T(8,128)(2,1)} async-done(((bf16[3,256,256]{1,2,0:T(8,128)(2,1)}), bf16[3,2048,256]{1,2,0:T(8,128)(2,1)}) %all-gather.8.cloned.1.call-update) | async-done | bytes 3145744 | tf_op jit(solution)/shard_map/all_gather | solution.py:79
  91.8 4.3 fusion.5
  98.7 18.5 %all-gather.10.cloned.1.call-done = bf16[256,2048]{1,0:T(8,128)(2,1)} async-done(((bf16[256,256]{1,0:T(8,128)(2,1)}), bf16[256,2048]{1,0:T(8,128)(2,1)}) %all-gather.10.cloned.1.call-update) | async-done | bytes 1048592 | tf_op jit(solution)/shard_map/all_gather | solution.py:88
  117.2 3.3 convolution_convert_fusion
  121.3 43.1 %reduce-scatter.3.cloned.1.call-done = bf16[128,2048]{1,0:T(8,128)(2,1)} async-done(((bf16[512,2048]{1,0:T(8,128)(2,1)}), bf16[128,2048]{1,0:T(8,128)(2,1)}) %reduce-scatter.3.cloned.1.call-update) | async-done | bytes 524304 | tf_op jit(solution)/shard_map/reduce_scatter | solution.py:90
  167.3 2.2 multiply_convert_fusion.1
  170.3 2.6 collective-permute-start
  172.9 44.4 %collective-permute-done.1 = bf16[2,256,2048]{2,1,0:T(8,128)(2,1)S(1)} collective-permute-done((bf16[2,256,2048]{2,1,0:T(8,128)(2,1)S(1)}, bf16[2,256,2048]{2,1,0:T(8,128)(2,1)S(1)}, u32[]{:S(2)}, u32[]{:S(2)}) %collective-permute-start.1) | collective-permute-done | bytes 2097184 | tf_op jit(solution)/shard_map/ppermute | solution.py:17
  220.1 75.3 %collective-permute-done.3 = bf16[2,256,2048]{2,1,0:T(8,128)(2,1)} collective-permute-done((bf16[2,256,2048]{2,1,0:T(8,128)(2,1)S(1)}, bf16[2,256,2048]{2,1,0:T(8,128)(2,1)}, u32[]{:S(2)}, u32[]{:S(2)}) %collective-permute-start.3) | collective-permute-done | bytes 2097184 | tf_op jit(solution)/shard_map/ppermute | solution.py:17
  295.4 3.6 collective-permute-done.2
  299.0 2.8 collective-permute-start.4
  301.8 39.8 %collective-permute-done.5 = bf16[2,256,2048]{2,1,0:T(8,128)(2,1)} collective-permute-done((bf16[2,256,2048]{2,1,0:T(8,128)(2,1)}, bf16[2,256,2048]{2,1,0:T(8,128)(2,1)}, u32[]{:S(2)}, u32[]{:S(2)}) %collective-permute-start.5) | collective-permute-done | bytes 2097184 | tf_op jit(solution)/shard_map/ppermute | solution.py:17
  341.7 6.3 %fusion.33 = f32[512,2,2048]{2,0,1:T(8,128)} fusion(bf16[2,256,2048]{2,1,0:T(8,128)(2,1)} %collective-permute-done.3, bf16[512,2048]{1,0:T(8,128)(2,1)} %all-gather.12.cloned.1.call-done, s32[]{:T(128)S(6)} %select_n.73), kind=kOutput, calls=%fused_computation.58 | convolution fusion | flops 1073741824 | bytes 10747908 | tf_op jit(solution)/shard_map/td,cdf->tcf/dot_general | solution.py:106
  348.0 6.2 %fusion.35 = f32[512,2,2048]{2,0,1:T(8,128)} fusion(bf16[2,256,2048]{2,1,0:T(8,128)(2,1)} %collective-permute-done.2, bf16[512,2048]{1,0:T(8,128)(2,1)S(1)} %copy-done.7, s32[]{:T(128)S(6)} %select_n.71), kind=kOutput, calls=%fused_computation.60 | convolution fusion | flops 1073741824 | bytes 10747908 | tf_op jit(solution)/shard_map/td,cdf->tcf/dot_general | solution.py:106
  354.2 4.5 fusion.37
  358.7 6.1 %fusion.39 = f32[512,2,2048]{2,0,1:T(8,128)} fusion(bf16[2,256,2048]{2,1,0:T(8,128)(2,1)} %collective-permute-done, bf16[512,2048]{1,0:T(8,128)(2,1)S(1)} %copy-done.7, s32[]{:T(128)S(6)} %select_n.67), kind=kOutput, calls=%fused_computation.64 | convolution fusion | flops 1073741824 | bytes 10747908 | tf_op jit(solution)/shard_map/td,cdf->tcf/dot_general | solution.py:106
  364.8 6.1 %fusion.29 = f32[512,2,2048]{2,0,1:T(8,128)} fusion(bf16[2,256,2048]{2,1,0:T(8,128)(2,1)} %collective-permute-done.5, bf16[512,2048]{1,0:T(8,128)(2,1)S(1)} %copy-done.7, s32[]{:T(128)S(6)} %select_n.77), kind=kOutput, calls=%fused_computation.54 | convolution fusion | flops 1073741824 | bytes 10747908 | tf_op jit(solution)/shard_map/td,cdf->tcf/dot_general | solution.py:106
  370.9 4.5 fusion.41
  375.3 6.1 %fusion.31 = f32[512,2,2048]{2,0,1:T(8,128)} fusion(bf16[2,256,2048]{2,1,0:T(8,128)(2,1)} %collective-permute-done.4, bf16[512,2048]{1,0:T(8,128)(2,1)S(1)} %copy-done.7, s32[]{:T(128)S(6)} %select_n.75), kind=kOutput, calls=%fused_computation.56 | convolution fusion | flops 1073741824 | bytes 10747908 | tf_op jit(solution)/shard_map/td,cdf->tcf/dot_general | solution.py:106
  381.4 23.6 %add_add_fusion = f32[512,2,2048]{2,0,1:T(8,128)} fusion(f32[512,2,2048]{2,0,1:T(8,128)} %fusion.29, f32[512,2,2048]{2,0,1:T(8,128)} %fusion.31, f32[512,2,2048]{2,0,1:T(8,128)} %fusion.33, f32[512,2,2048]{2,0,1:T(8,128)} %fusion.35, f32[512,2,2048]{2,0,1:T(8,128)} %fusion.37, f32[512,2,2048]{2,0,1:T(8,128)} %fusion.41, f32[512,2,2048]{2,0,1:T(8,128)} %fusion.39, ...), kind=kOutput, calls=%fused_computation.1 | convolution fusion | flops 1088421888 | bytes 69468160 | tf_op jit(solution)/shard_map/td,cdf->tcf/dot_general | solution.py:106
  405.0 12.0 %convolution_convert_fusion.1 = bf16[512,2048]{1,0:T(8,128)(2,1)} fusion(bf16[2048,2048]{1,0:T(8,128)(2,1)} %all-gather.14.cloned.1.call-done, f32[512,2,2048]{2,0,1:T(8,128)} %add_add_fusion, f32[2048]{0:T(1024)S(1)} %bitcast.117, f32[2048]{0:T(1024)S(1)} %bitcast.116), kind=kOutput, calls=%fused_computation.9 | convolution fusion | flops 4304404480 | bytes 18890752 | tf_op jit(solution)/shard_map/dot_general | solution.py:119
  417.0 50.1 %reduce-scatter.5.cloned.1.call-done = bf16[128,2048]{1,0:T(8,128)(2,1)} async-done(((bf16[512,2048]{1,0:T(8,128)(2,1)}), bf16[128,2048]{1,0:T(8,128)(2,1)}) %reduce-scatter.5.cloned.1.call-update) | async-done | bytes 524304 | tf_op jit(solution)/shard_map/reduce_scatter | solution.py:118
  469.8 2.3 fusion.20
  (66 shorter events, 17.6 us)
Async XLA Ops:
  6.5 5.1 %copy-start = (f32[1024]{0:T(1024)S(1)}, f32[1024]{0:T(1024)}, u32[]{:S(2)}) copy-start(f32[1024]{0:T(1024)} %param.10) | copy-start | bytes 12292
  6.5 3.4 copy-start.8
  6.5 51.8 %all-gather.6.cloned.1.call-start = ((), (), s32[]{:S(2)}) async-start(), calls=%async_computation.2 | async-start | bytes 2621440 | tf_op jit(solution)/shard_map/all_gather | solution.py:73
  9.8 82.0 %all-gather.8.cloned.1.call-start = ((), (), s32[]{:S(2)}) async-start(), calls=%async_computation.3 | async-start | bytes 3538944 | tf_op jit(solution)/shard_map/all_gather | solution.py:79
  10.9 106.4 %all-gather.10.cloned.1.call-start = ((), (), s32[]{:S(2)}) async-start(), calls=%async_computation.4 | async-start | bytes 1179648 | tf_op jit(solution)/shard_map/all_gather | solution.py:88
  11.6 152.8 %reduce-scatter.3.cloned.1.call-start = ((), (), s32[]{:S(2)}) async-start(), calls=%async_computation.5 | async-start | bytes 2621440 | tf_op jit(solution)/shard_map/reduce_scatter | solution.py:90
  120.5 45.1 %copy-start.2 = (bf16[1,128,2048]{2,1,0:T(8,128)(2,1)S(1)}, bf16[1,128,2048]{2,1,0:T(8,128)(2,1)}, u32[]{:S(2)}) copy-start(bf16[1,128,2048]{2,1,0:T(8,128)(2,1)} %param.8) | copy-start | bytes 1572868
  120.6 221.1 %all-gather.12.cloned.1.call-start = ((), (), s32[]{:S(2)}) async-start(), calls=%async_computation.6 | async-start | bytes 2621440 | tf_op jit(solution)/shard_map/all_gather | solution.py:100
  165.6 4.6 copy-start.4
  165.6 129.8 %copy-start.10 = (f32[2,2048]{1,0:T(2,128)S(1)}, f32[2,2048]{1,0:T(2,128)}, u32[]{:S(2)}) copy-start(f32[2,2048]{1,0:T(2,128)} %param.14) | copy-start | bytes 49156
  169.6 235.5 %all-gather.14.cloned.1.call-start = ((), (), s32[]{:S(2)}) async-start(), calls=%async_computation.7 | async-start | bytes 9437184 | tf_op jit(solution)/shard_map/all_gather | solution.py:116
  170.1 297.0 %reduce-scatter.5.cloned.1.call-start = ((), (), s32[]{:S(2)}) async-start(), calls=%async_computation.8 | async-start | bytes 2621440 | tf_op jit(solution)/shard_map/reduce_scatter | solution.py:118
  170.2 47.1 %collective-permute-start.1 = (bf16[2,256,2048]{2,1,0:T(8,128)(2,1)S(1)}, bf16[2,256,2048]{2,1,0:T(8,128)(2,1)S(1)}, u32[]{:S(2)}, u32[]{:S(2)}) collective-permute-start(bf16[2,256,2048]{2,1,0:T(8,128)(2,1)S(1)} %copy-done.4), channel_id=1, source_target_pairs={{0,4},{4,8},{8,12},{12,16},{16,20},{20,24},{24,28},{28,0},{1,5},{5... | collective-permute-start | bytes 6291464 | tf_op jit(solution)/shard_map/ppermute | solution.py:17
  170.3 47.0 %collective-permute-start = (bf16[2,256,2048]{2,1,0:T(8,128)(2,1)S(1)}, bf16[2,256,2048]{2,1,0:T(8,128)(2,1)}, u32[]{:S(2)}, u32[]{:S(2)}) collective-permute-start(bf16[2,256,2048]{2,1,0:T(8,128)(2,1)S(1)} %copy-done.4), channel_id=1, source_target_pairs={{0,28},{4,0},{8,4},{12,8},{16,12},{20,16},{24,20},{28,24},{1,29},{... | collective-permute-start | bytes 6291464 | tf_op jit(solution)/shard_map/ppermute | solution.py:19
  217.3 1.3 copy-start.5
  217.3 78.1 %collective-permute-start.3 = (bf16[2,256,2048]{2,1,0:T(8,128)(2,1)S(1)}, bf16[2,256,2048]{2,1,0:T(8,128)(2,1)}, u32[]{:S(2)}, u32[]{:S(2)}) collective-permute-start(bf16[2,256,2048]{2,1,0:T(8,128)(2,1)S(1)} %collective-permute-done.1), channel_id=1, source_target_pairs={{0,4},{4,8},{8,12},{12,16},{16,20},{20,24},{24,28},{28,0},{1,5},{5... | collective-permute-start | bytes 6291464 | tf_op jit(solution)/shard_map/ppermute | solution.py:17
  218.6 80.4 %collective-permute-start.2 = (bf16[2,256,2048]{2,1,0:T(8,128)(2,1)}, bf16[2,256,2048]{2,1,0:T(8,128)(2,1)}, u32[]{:S(2)}, u32[]{:S(2)}) collective-permute-start(bf16[2,256,2048]{2,1,0:T(8,128)(2,1)} %collective-permute-done), channel_id=1, source_target_pairs={{0,28},{4,0},{8,4},{12,8},{16,12},{20,16},{24,20},{28,24},{1,29},{... | collective-permute-start | bytes 6291464 | tf_op jit(solution)/shard_map/ppermute | solution.py:19
  295.4 46.3 %collective-permute-start.5 = (bf16[2,256,2048]{2,1,0:T(8,128)(2,1)}, bf16[2,256,2048]{2,1,0:T(8,128)(2,1)}, u32[]{:S(2)}, u32[]{:S(2)}) collective-permute-start(bf16[2,256,2048]{2,1,0:T(8,128)(2,1)} %collective-permute-done.3), channel_id=1, source_target_pairs={{0,4},{4,8},{8,12},{12,16},{16,20},{20,24},{24,28},{28,0},{1,5},{5... | collective-permute-start | bytes 6291464 | tf_op jit(solution)/shard_map/ppermute | solution.py:17
  299.0 76.3 %collective-permute-start.4 = (bf16[2,256,2048]{2,1,0:T(8,128)(2,1)}, bf16[2,256,2048]{2,1,0:T(8,128)(2,1)}, u32[]{:S(2)}, u32[]{:S(2)}) collective-permute-start(bf16[2,256,2048]{2,1,0:T(8,128)(2,1)} %collective-permute-done.2), channel_id=1, source_target_pairs={{0,28},{4,0},{8,4},{12,8},{16,12},{20,16},{24,20},{28,24},{1,29},{... | collective-permute-start | bytes 6291464 | tf_op jit(solution)/shard_map/ppermute | solution.py:19
  341.7 39.7 %collective-permute-start.6 = (bf16[2,256,2048]{2,1,0:T(8,128)(2,1)}, bf16[2,256,2048]{2,1,0:T(8,128)(2,1)}, u32[]{:S(2)}, u32[]{:S(2)}) collective-permute-start(bf16[2,256,2048]{2,1,0:T(8,128)(2,1)} %collective-permute-done.5), channel_id=1, source_target_pairs={{0,4},{4,8},{8,12},{12,16},{16,20},{20,24},{24,28},{28,0},{1,5},{5... | collective-permute-start | bytes 6291464 | tf_op jit(solution)/shard_map/ppermute | solution.py:17
  341.7 6.3 %copy-start.7 = (bf16[512,2048]{1,0:T(8,128)(2,1)S(1)}, bf16[512,2048]{1,0:T(8,128)(2,1)}, u32[]{:S(2)}) copy-start(bf16[512,2048]{1,0:T(8,128)(2,1)} %all-gather.12.cloned.1.call-done) | copy-start | bytes 6291460
  348.0 6.2 %copy-start.6 = (bf16[2,256,2048]{2,1,0:T(8,128)(2,1)S(1)}, bf16[2,256,2048]{2,1,0:T(8,128)(2,1)}, u32[]{:S(2)}) copy-start(bf16[2,256,2048]{2,1,0:T(8,128)(2,1)} %copy-done.5) | copy-start | bytes 6291460
  417.0 51.4 %copy-start.3 = (bf16[128,2048]{1,0:T(8,128)(2,1)S(1)}, bf16[128,2048]{1,0:T(8,128)(2,1)}, u32[]{:S(2)}) copy-start(bf16[128,2048]{1,0:T(8,128)(2,1)} %multiply_convert_fusion.1) | copy-start | bytes 1572868
  417.0 55.2 %copy-start.1 = (f32[1024]{0:T(1024)S(1)}, f32[1024]{0:T(1024)}, u32[]{:S(2)}) copy-start(f32[1024]{0:T(1024)} %param.10) | copy-start | bytes 12292
  (1 other events, 0.7 us)
Sparse Core Ops, SparseCore 0:
  10.0 48.3 all-gather.5
  60.3 31.5 all-gather.7
  93.7 23.4 all-gather.9
  120.7 43.6 reduce-scatter.2
  169.7 44.8 all-gather.11
  216.3 86.5 all-gather.13
  417.1 49.9 reduce-scatter.4
